TPU v7x, 512 devices: a whole 4x4x16 slice. The times are simulated.
512 devices in a mesh: dp: 64 (over y, z), mp: 8 (over x, core).
Axes of the slice: x: 4, y: 4, z: 16, core: 2. Of those that a mesh axis runs over, the one named last changes fastest.
Arguments:
- tokens: bfloat16 [512, 8192], P('mp', 'dp'), may hold values from -6 to 6
- norm_gain: float32 [8192], replicated, may hold values from 0.25 to 1.75
- query_weight: bfloat16 [8192, 8192], P(None, 'dp'), may hold values from -0.0625 to 0.0625
- out_weight: bfloat16 [8192, 8192], P(None, 'dp'), may hold values from -0.0625 to 0.0625
- gate_scalar: float32 [1], replicated, may hold values from 0.4 to 1.5
- image_keys: bfloat16 [128, 64, 8192], P('mp', None, 'dp'), may hold values from -260 to 260
- image_values: bfloat16 [128, 64, 8192], P('mp', None, 'dp'), may hold values from -6 to 6
- active_image: int32 [128, 4], replicated, may hold values from 0 to 127
- image_slot: int32 [128], replicated, may hold values from 0 to 127, each once
Outputs:
- mixed: bfloat16 [512, 8192], P('mp', 'dp')
Inputs may be any that keep to these rules, and one draw needn't show every extreme that they name: `image_slot`: each slot 0 to 127 once.
All inputs are finite; a program needn't handle non-finite values.
Results may differ from a plain program's by a relative error of at most 0.0047.
Values may be sent and summed in bfloat16 or wider, within the bound.
A program may use at most 64 MiB of HBM per device.

v0:
```python
import jax
import jax.numpy as jnp
from jax import lax
from jax.sharding import Mesh
from jax.sharding import PartitionSpec as P

DP = ("dp_0", "dp_1")
epsilon = 1e-05


def laid_out(parts, dim):
    lengths = list(parts.shape[1:])
    lengths[dim] *= parts.shape[0]
    return jnp.moveaxis(parts, 0, dim).reshape(lengths)


def gather_in_order(value, axes, sequence):
    parts = value[None]
    for k in sequence:
        parts = lax.all_gather(parts, axes[k], axis=0, tiled=True)
    carried = [lax.axis_size(axes[k]) for k in reversed(sequence)]
    parts = parts.reshape(*carried, *value.shape)
    turned = sorted(range(len(sequence)), key=lambda place: sequence[len(sequence) - 1 - place])
    return parts.transpose(*turned, *range(len(sequence), parts.ndim)).reshape(-1, *value.shape)


def whole_of(value, axes, sequence, dim):
    return laid_out(gather_in_order(value, axes, sequence), dim)


def from_everyone(value, axis):
    copies = jnp.broadcast_to(value, (lax.axis_size(axis), *value.shape))
    return lax.all_to_all(copies, axis, split_axis=0, concat_axis=0, tiled=True)


def gathered_copies(value, axis, dim):
    parts = from_everyone(value, axis)
    return laid_out(parts, dim)


def split_up(value, dim, peers):
    lengths = value.shape
    parts = value.reshape(*lengths[:dim], peers, lengths[dim] // peers, *lengths[dim + 1 :])
    return jnp.moveaxis(parts, dim, 0)


def sent_and_summed(value, axis, dim):
    peers = lax.axis_size(axis)
    parts = lax.all_to_all(split_up(value, dim, peers), axis, 0, 0, tiled=True)
    return jnp.sum(parts.astype(jnp.float32), axis=0)


def attend(queries, wanted, keys_block, values_block, first_slot):
    visual = keys_block.shape[1]
    width = keys_block.shape[2]
    flat_keys = keys_block.reshape(-1, width)
    flat_values = values_block.reshape(-1, width)
    scores = lax.dot_general(
        queries, flat_keys, (((1,), (1,)), ((), ())), preferred_element_type=jnp.float32
    ) * width ** (-0.5)
    column_slot = first_slot + jnp.arange(flat_keys.shape[0], dtype=jnp.int32) // visual
    matches = wanted[:, None] == column_slot[None, :]
    owned = jnp.any(matches, axis=1, keepdims=True)
    masked = jnp.where(matches, scores, -1e30)
    largest = jnp.max(masked, axis=1, keepdims=True)
    expo = jnp.where(matches, jnp.exp(masked - largest), 0.0)
    totals = jnp.where(owned, jnp.sum(expo, axis=1, keepdims=True), 1.0)
    rounded = (expo / totals).astype(jnp.bfloat16)
    result = jnp.dot(rounded, flat_values, preferred_element_type=jnp.float32)
    return jnp.where(owned, result, 0.0)


def body(
    tokens,
    norm_gain,
    query_weight,
    out_weight,
    gate_scalar,
    image_keys,
    image_values,
    active_image,
    image_slot,
):
    whole = whole_of(tokens, DP, (0, 1), 1)
    widened = whole.astype(jnp.float32)
    average = jnp.mean(widened, axis=1, keepdims=True)
    centred = widened - average
    variance = jnp.mean(centred * centred, axis=1, keepdims=True)
    normed = (centred * lax.rsqrt(variance + epsilon) * norm_gain).astype(jnp.bfloat16)
    queries = jnp.dot(normed, query_weight, preferred_element_type=jnp.float32).astype(jnp.bfloat16)
    slots_all = image_slot[active_image.reshape(-1)]
    owned_slots = image_keys.shape[0]
    every_query = gathered_copies(queries, "mp", 0)
    first_slot = lax.axis_index("mp") * owned_slots
    gathered = sent_and_summed(
        attend(every_query, slots_all, image_keys, image_values, first_slot).astype(jnp.bfloat16),
        "mp",
        0,
    )
    attended = gathered.astype(jnp.bfloat16)
    projected = jnp.dot(
        whole_of(attended, DP, (0, 1), 1), out_weight, preferred_element_type=jnp.float32
    )
    result = tokens.astype(jnp.float32) + jnp.tanh(gate_scalar[0]) * projected
    return result.astype(jnp.bfloat16)


def solution(mesh):
    split = Mesh(mesh.devices.reshape(4, 16, mesh.shape["mp"]), ("dp_0", "dp_1", "mp"))
    placed = (
        P("mp", DP),
        P(),
        P(None, DP),
        P(None, DP),
        P(),
        P("mp", None, DP),
        P("mp", None, DP),
        P(),
        P(),
    )
    return jax.shard_map(body, mesh=split, in_specs=placed, out_specs=P("mp", DP), check_vma=False)
```

profile of v0, /device:TPU:2, one launch (start us, length us, event | category | flops | bytes accessed | tf_op | source)
XLA Modules:
  0.0 209.5 jit_solution(14668221166612236900)
XLA Ops:
  6.5 14.0 %all-gather = bf16[256,128]{1,0:T(8,128)(2,1)} all-gather(bf16[64,128]{1,0:T(8,128)(2,1)} %param.9), channel_id=2, replica_groups=mesh['dp_0'=4,'dp_1'=16,'mp'=8] {'dp_0'}, dimensions={0}, use_global_device_ids=true | all-gather | bytes 81920 | tf_op jit(solution)/shard_map/all_gather | solution.py:20
  20.6 0.8 copy.18
  21.4 0.1 reshape.104
  21.5 3.4 %gather_fusion = s32[512]{0:T(512)S(1)} fusion(s32[128]{0:T(128)} %param.17, s32[1024]{0:T(1024)S(1)} %pad_clamp_fusion), kind=kCustom, calls=%fused_computation | custom fusion | bytes 6144 | tf_op jit(solution)/shard_map/gather | solution.py:91
  25.0 69.7 %all-gather.5.cloned.1.call-done = bf16[64,64,128]{2,1,0:T(8,128)(2,1)} async-done(((bf16[4,64,128]{2,1,0:T(8,128)(2,1)}), bf16[64,64,128]{2,1,0:T(8,128)(2,1)}) %all-gather.5.cloned.1.call-update) | async-done | bytes 1048592 | tf_op jit(solution)/shard_map/all_gather | solution.py:20
  94.6 1.5 convert_reduce_fusion
  96.1 1.5 convert_element_type.65
  97.6 0.2 copy.19
  97.9 0.4 fusion.4
  98.3 0.3 copy-done.3
  98.6 0.6 convolution_convert_fusion
  99.2 0.7 broadcast_in_dim.43
  99.9 4.8 %all-to-all-start = ((bf16[8,64,128]{2,1,0:T(8,128)(2,1)}), bf16[8,64,128]{2,1,0:T(8,128)(2,1)S(1)}, u32[]{:S(2)}, u32[]{:S(2)}) async-start(bf16[8,64,128]{2,1,0:T(8,128)(2,1)} %broadcast_in_dim.43), calls=%async_computation | async-start | bytes 262144 | tf_op jit(solution)/shard_map/all_to_all | solution.py:33
  104.7 0.4 compare_reduce_fusion
  105.1 4.3 %all-to-all-done = bf16[8,64,128]{2,1,0:T(8,128)(2,1)S(1)} async-done(((bf16[8,64,128]{2,1,0:T(8,128)(2,1)}), bf16[8,64,128]{2,1,0:T(8,128)(2,1)S(1)}, u32[]{:S(2)}, u32[]{:S(2)}) %all-to-all-start) | async-done | bytes 131104 | tf_op jit(solution)/shard_map/all_to_all | solution.py:33
  109.3 0.5 fusion.5
  109.9 0.7 fusion.6
  110.6 1.2 fusion.7
  111.8 8.5 %all_to_all.10 = bf16[8,64,128]{2,1,0:T(8,128)(2,1)S(1)} all-to-all(bf16[8,64,128]{2,1,0:T(8,128)(2,1)S(1)} %bitcast.51), channel_id=1, replica_groups=mesh['dp_0'=4,'dp_1'=16,'mp'=8] {'mp'}, dimensions={0} | all-to-all | bytes 262144 | tf_op jit(solution)/shard_map/all_to_all | solution.py:49
  120.4 12.9 %all-gather.1 = bf16[256,128]{1,0:T(8,128)(2,1)} all-gather(bf16[64,128]{1,0:T(8,128)(2,1)S(1)} %reduce_sum.42), channel_id=3, replica_groups=mesh['dp_0'=4,'dp_1'=16,'mp'=8] {'dp_0'}, dimensions={0}, use_global_device_ids=true | all-gather | bytes 81920 | tf_op jit(solution)/shard_map/all_gather | solution.py:20
  134.0 65.6 %all-gather.7.cloned.1.call-done = bf16[64,64,128]{2,1,0:T(8,128)(2,1)} async-done(((bf16[4,64,128]{2,1,0:T(8,128)(2,1)}), bf16[64,64,128]{2,1,0:T(8,128)(2,1)}) %all-gather.7.cloned.1.call-update) | async-done | bytes 1048592 | tf_op jit(solution)/shard_map/all_gather | solution.py:20
  199.6 1.5 copy.21
  201.1 0.4 copy-done.1
  201.5 1.1 fusion.9
  (21 shorter events, 0.1 us)
Async XLA Ops:
  6.5 91.8 %copy-start = (bf16[8192,128]{1,0:T(8,128)(2,1)S(1)}, bf16[8192,128]{1,0:T(8,128)(2,1)}, u32[]{:S(2)}) copy-start(bf16[8192,128]{1,0:T(8,128)(2,1)} %param.11) | copy-start | bytes 6291460
  6.5 88.1 %all-gather.5.cloned.1.call-start = ((), (), s32[]{:S(2)}) async-start(), calls=%async_computation.2 | async-start | bytes 1114112 | tf_op jit(solution)/shard_map/all_gather | solution.py:20
  97.9 0.8 copy-start.3
  98.6 10.7 %copy-start.4 = (bf16[16,64,128]{2,1,0:T(8,128)(2,1)S(1)}, bf16[16,64,128]{2,1,0:T(8,128)(2,1)}, u32[]{:S(2)}) copy-start(bf16[16,64,128]{2,1,0:T(8,128)(2,1)} %param.14) | copy-start | bytes 786436
  99.9 9.4 %all-to-all-start = ((bf16[8,64,128]{2,1,0:T(8,128)(2,1)}), bf16[8,64,128]{2,1,0:T(8,128)(2,1)S(1)}, u32[]{:S(2)}, u32[]{:S(2)}) async-start(bf16[8,64,128]{2,1,0:T(8,128)(2,1)} %broadcast_in_dim.43), calls=%async_computation | async-start | bytes 262144 | tf_op jit(solution)/shard_map/all_to_all | solution.py:33
  104.7 95.0 %all-gather.7.cloned.1.call-start = ((), (), s32[]{:S(2)}) async-start(), calls=%async_computation.3 | async-start | bytes 1114112 | tf_op jit(solution)/shard_map/all_gather | solution.py:20
  109.3 1.3 copy-start.5
  111.8 89.3 %copy-start.2 = (bf16[64,128]{1,0:T(8,128)(2,1)S(1)}, bf16[64,128]{1,0:T(8,128)(2,1)}, u32[]{:S(2)}) copy-start(bf16[64,128]{1,0:T(8,128)(2,1)} %param.9) | copy-start | bytes 49156
  199.6 1.9 copy-start.1
Sparse Core Ops, SparseCore 0:
  20.7 73.8 all-gather.4
  133.4 66.1 all-gather.6
where the time goes:
time: 210 us
  waiting for transfers between devices  140 us (67%)
  blocking collectives  35.5 us (17%)
  between operations  14.2 us (7%)
  local copies, waits for them, and re-layouts  7.49 us (4%)
  starting transfers between devices  4.81 us (2%)
  other arithmetic  4.52 us (2%)
  matrix products  3.47 us (2%)
    all_gather x2, waiting for transfers between devices, gather_in_order(): parts = lax.all_gather(parts, axes[k], axis=0, tiled=True)  135 us
    all_gather x2, blocking collectives, gather_in_order(): parts = lax.all_gather(parts, axes[k], axis=0, tiled=True)  27 us
    all_to_all x1, blocking collectives, sent_and_summed(): parts = lax.all_to_all(split_up(value, dim, peers), axis, 0, 0, tiled=True)  8.49 us
    all_to_all x1, starting transfers between devices, from_everyone(): return lax.all_to_all(copies, axis, split_axis=0, concat_axis=0, tiled=True)  4.8 us
    all_to_all x1, waiting for transfers between devices, from_everyone(): return lax.all_to_all(copies, axis, split_axis=0, concat_axis=0, tiled=True)  4.26 us
  transfers between devices with their start and end apart: 3, of which 3 were waited for; matrix products, arithmetic and copies ran while one was open for 2% of the time, Pallas kernels for 0%

commit v1 on v0

--- a/solution.py
+++ b/solution.py
@@ -17,7 +17,10 @@
 def gather_in_order(value, axes, sequence):
     parts = value[None]
     for k in sequence:
-        parts = lax.all_gather(parts, axes[k], axis=0, tiled=True)
+        devices = lax.axis_size(axes[k])
+        shards = jnp.stack([parts for _ in range(devices)])
+        shards = lax.all_to_all(shards, axes[k], split_axis=0, concat_axis=0)
+        parts = jnp.concatenate(shards, axis=0)
     carried = [lax.axis_size(axes[k]) for k in reversed(sequence)]
     parts = parts.reshape(*carried, *value.shape)
     turned = sorted(range(len(sequence)), key=lambda place: sequence[len(sequence) - 1 - place])

time: 210 us -> 168 us (0.80)
  the two profiles are of different devices: /device:TPU:2 before, /device:TPU:64 now
where the time goes in v1:
time: 168 us; the launch traced here: 167 us
  waiting for transfers between devices  97.1 us (58%)
  starting transfers between devices  27.7 us (16%)
  blocking collectives  26.5 us (16%)
  local copies, waits for them, and re-layouts  9.28 us (6%)
  matrix products  3.47 us (2%)
  other arithmetic  2.05 us (1%)
    all_to_all x2, waiting for transfers between devices, gather_in_order(): shards = lax.all_to_all(shards, axes[k], split_axis=0, concat_axis=0)  91.4 us
    all_to_all x2, starting transfers between devices, gather_in_order(): shards = lax.all_to_all(shards, axes[k], split_axis=0, concat_axis=0)  23.4 us
    all_to_all x2, blocking collectives, gather_in_order(): shards = lax.all_to_all(shards, axes[k], split_axis=0, concat_axis=0)  18 us
    all_to_all x1, blocking collectives, sent_and_summed(): parts = lax.all_to_all(split_up(value, dim, peers), axis, 0, 0, tiled=True)  8.49 us
    all_to_all x1, waiting for transfers between devices, from_everyone(): return lax.all_to_all(copies, axis, split_axis=0, concat_axis=0, tiled=True)  5.72 us
    all_to_all x1, starting transfers between devices, from_everyone(): return lax.all_to_all(copies, axis, split_axis=0, concat_axis=0, tiled=True)  4.3 us
    another operation x4, local copies, waits for them, and re-layouts, gather_in_order(): shards = jnp.stack([parts for _ in range(devices)])  3.37 us
  transfers between devices with their start and end apart: 3, of which 3 were waited for; matrix products, arithmetic and copies ran while one was open for 2% of the time, Pallas kernels for 0%

profile of v1, /device:TPU:64, one launch (start us, length us, event | category | flops | bytes accessed | tf_op | source)
XLA Modules:
  0.0 166.9 jit_solution(5476381421377671626)
XLA Ops:
  0.0 0.9 stack.12
  0.9 9.9 %all_to_all.30 = bf16[4,1,64,128]{3,2,1,0:T(8,128)(2,1)S(1)} all-to-all(bf16[4,1,64,128]{3,2,1,0:T(8,128)(2,1)S(1)} %stack.12), channel_id=1, replica_groups=mesh['dp_0'=4,'dp_1'=16,'mp'=8] {'dp_0'}, dimensions={0} | all-to-all | bytes 131072 | tf_op jit(solution)/shard_map/all_to_all | solution.py:22
  10.8 1.2 stack.13
  12.0 14.8 %all-to-all-start.1 = ((bf16[16,4,64,128]{3,2,1,0:T(8,128)(2,1)}), bf16[16,4,64,128]{3,2,1,0:T(8,128)(2,1)S(1)}, u32[]{:S(2)}, u32[]{:S(2)}) async-start(bf16[16,4,64,128]{3,2,1,0:T(8,128)(2,1)} %stack.13), calls=%async_computation.1 | async-start | bytes 2097152 | tf_op jit(solution)/shard_map/all_to_all | solution.py:22
  27.0 3.3 %gather_fusion = s32[512]{0:T(512)S(1)} fusion(s32[128]{0:T(128)S(1)} %copy-done.1, s32[1024]{0:T(1024)S(1)} %pad_clamp_fusion), kind=kCustom, calls=%fused_computation | custom fusion | bytes 6144 | tf_op jit(solution)/shard_map/gather | solution.py:94
  30.4 44.2 %all-to-all-done.1 = bf16[16,4,64,128]{3,2,1,0:T(8,128)(2,1)S(1)} async-done(((bf16[16,4,64,128]{3,2,1,0:T(8,128)(2,1)}), bf16[16,4,64,128]{3,2,1,0:T(8,128)(2,1)S(1)}, u32[]{:S(2)}, u32[]{:S(2)}) %all-to-all-start.1) | async-done | bytes 1048608 | tf_op jit(solution)/shard_map/all_to_all | solution.py:22
  74.6 0.3 fusion.16
  74.9 0.2 copy_convert_fusion
  75.1 0.4 fusion.4
  75.6 0.6 convolution_convert_fusion
  76.2 0.7 broadcast_in_dim.36
  76.8 4.3 %all-to-all-start.2 = ((bf16[8,64,128]{2,1,0:T(8,128)(2,1)}), bf16[8,64,128]{2,1,0:T(8,128)(2,1)S(1)}, u32[]{:S(2)}, u32[]{:S(2)}) async-start(bf16[8,64,128]{2,1,0:T(8,128)(2,1)} %broadcast_in_dim.36), calls=%async_computation.2 | async-start | bytes 262144 | tf_op jit(solution)/shard_map/all_to_all | solution.py:36
  81.1 0.4 compare_reduce_fusion
  81.5 5.7 %all-to-all-done.2 = bf16[8,64,128]{2,1,0:T(8,128)(2,1)S(1)} async-done(((bf16[8,64,128]{2,1,0:T(8,128)(2,1)}), bf16[8,64,128]{2,1,0:T(8,128)(2,1)S(1)}, u32[]{:S(2)}, u32[]{:S(2)}) %all-to-all-start.2) | async-done | bytes 131104 | tf_op jit(solution)/shard_map/all_to_all | solution.py:36
  87.2 0.5 fusion.5
  87.8 0.7 fusion.6
  88.5 1.2 fusion.7
  89.7 8.5 %all_to_all.31 = bf16[8,64,128]{2,1,0:T(8,128)(2,1)S(1)} all-to-all(bf16[8,64,128]{2,1,0:T(8,128)(2,1)S(1)} %bitcast.47), channel_id=1, replica_groups=mesh['dp_0'=4,'dp_1'=16,'mp'=8] {'mp'}, dimensions={0} | all-to-all | bytes 262144 | tf_op jit(solution)/shard_map/all_to_all | solution.py:52
  98.3 8.2 %all_to_all.32 = bf16[4,1,64,128]{3,2,1,0:T(8,128)(2,1)S(1)} all-to-all(bf16[4,1,64,128]{3,2,1,0:T(8,128)(2,1)S(1)} %stack.14), channel_id=1, replica_groups=mesh['dp_0'=4,'dp_1'=16,'mp'=8] {'dp_0'}, dimensions={0} | all-to-all | bytes 131072 | tf_op jit(solution)/shard_map/all_to_all | solution.py:22
  106.4 1.2 stack.15
  107.7 8.6 %all-to-all-start.5 = ((bf16[16,4,64,128]{3,2,1,0:T(8,128)(2,1)}), bf16[16,4,64,128]{3,2,1,0:T(8,128)(2,1)S(1)}, u32[]{:S(2)}, u32[]{:S(2)}) async-start(bf16[16,4,64,128]{3,2,1,0:T(8,128)(2,1)} %stack.15), calls=%async_computation.5 | async-start | bytes 2097152 | tf_op jit(solution)/shard_map/all_to_all | solution.py:22
  117.0 47.2 %all-to-all-done.5 = bf16[16,4,64,128]{3,2,1,0:T(8,128)(2,1)S(1)} async-done(((bf16[16,4,64,128]{3,2,1,0:T(8,128)(2,1)}), bf16[16,4,64,128]{3,2,1,0:T(8,128)(2,1)S(1)}, u32[]{:S(2)}, u32[]{:S(2)}) %all-to-all-start.5) | async-done | bytes 1048608 | tf_op jit(solution)/shard_map/all_to_all | solution.py:22
  164.3 1.5 copy-done.2
  165.8 1.1 fusion.9
  (26 shorter events, 0.5 us)
Async XLA Ops:
  0.0 75.5 %copy-start = (bf16[8192,128]{1,0:T(8,128)(2,1)S(1)}, bf16[8192,128]{1,0:T(8,128)(2,1)}, u32[]{:S(2)}) copy-start(bf16[8192,128]{1,0:T(8,128)(2,1)} %param.11) | copy-start | bytes 6291460
  0.0 26.8 %copy-start.5 = (s32[128,4]{0,1:T(4,128)S(1)}, s32[128,4]{0,1:T(4,128)}, u32[]{:S(2)}) copy-start(s32[128,4]{0,1:T(4,128)} %param.16) | copy-start | bytes 6148
  0.0 27.0 %copy-start.1 = (s32[128]{0:T(128)S(1)}, s32[128]{0:T(128)}, u32[]{:S(2)}) copy-start(s32[128]{0:T(128)} %param.17) | copy-start | bytes 1540
  12.0 62.5 %all-to-all-start.1 = ((bf16[16,4,64,128]{3,2,1,0:T(8,128)(2,1)}), bf16[16,4,64,128]{3,2,1,0:T(8,128)(2,1)S(1)}, u32[]{:S(2)}, u32[]{:S(2)}) async-start(bf16[16,4,64,128]{3,2,1,0:T(8,128)(2,1)} %stack.13), calls=%async_computation.1 | async-start | bytes 2097152 | tf_op jit(solution)/shard_map/all_to_all | solution.py:22
  74.9 0.8 copy-start.4
  75.6 11.6 %copy-start.6 = (bf16[16,64,128]{2,1,0:T(8,128)(2,1)S(1)}, bf16[16,64,128]{2,1,0:T(8,128)(2,1)}, u32[]{:S(2)}) copy-start(bf16[16,64,128]{2,1,0:T(8,128)(2,1)} %param.14) | copy-start | bytes 786436
  76.8 10.4 %all-to-all-start.2 = ((bf16[8,64,128]{2,1,0:T(8,128)(2,1)}), bf16[8,64,128]{2,1,0:T(8,128)(2,1)S(1)}, u32[]{:S(2)}, u32[]{:S(2)}) async-start(bf16[8,64,128]{2,1,0:T(8,128)(2,1)} %broadcast_in_dim.36), calls=%async_computation.2 | async-start | bytes 262144 | tf_op jit(solution)/shard_map/all_to_all | solution.py:36
  87.2 1.3 copy-start.7
  107.7 56.6 %copy-start.3 = (bf16[64,128]{1,0:T(8,128)(2,1)S(1)}, bf16[64,128]{1,0:T(8,128)(2,1)}, u32[]{:S(2)}) copy-start(bf16[64,128]{1,0:T(8,128)(2,1)} %param.9) | copy-start | bytes 49156
  107.7 56.5 %all-to-all-start.5 = ((bf16[16,4,64,128]{3,2,1,0:T(8,128)(2,1)}), bf16[16,4,64,128]{3,2,1,0:T(8,128)(2,1)S(1)}, u32[]{:S(2)}, u32[]{:S(2)}) async-start(bf16[16,4,64,128]{3,2,1,0:T(8,128)(2,1)} %stack.15), calls=%async_computation.5 | async-start | bytes 2097152 | tf_op jit(solution)/shard_map/all_to_all | solution.py:22
  164.2 1.6 copy-start.2
